TPU v7x, 32 devices: a whole 2x2x4 slice. The times are simulated.
32 devices in a mesh: dp: 4 (over y, core), lat: 4 (over z), chan: 2 (over x).
Axes of the slice: x: 2, y: 2, z: 4, core: 2. Of those that a mesh axis runs over, the one named last changes fastest.
Arguments:
- saved_input: bfloat16 [4, 16, 720, 1024], P('dp', None, 'lat', 'chan'), may hold values from -6 to 6
- grad_output: bfloat16 [4, 16, 720, 1024], P('dp', None, 'lat', 'chan'), may hold values from -6 to 6
- legendre: bfloat16 [16, 192, 720], P('lat'), may hold values from -0.21875 to 0.21875
- quad_weight: float32 [720], replicated, may hold values from 0.3 to 3
- mixing_weight: bfloat16 [192, 512, 1024], P('lat', None, 'chan'), may hold values from -0.375 to 0.375
Outputs:
- grad_weight: bfloat16 [192, 512, 1024], P('lat', 'dp', 'chan')
- grad_input: bfloat16 [4, 16, 720, 1024], P('dp', None, 'lat', 'chan')
All inputs are finite; a program needn't handle non-finite values.
Results may differ from a plain program's by a relative error of at most 0.014.
Values may be sent and summed in bfloat16 or wider, within the bound.
A program may use at most 192 MiB of HBM per device.

v0:
```python
import jax
import jax.numpy as jnp
from jax import lax
from jax.sharding import PartitionSpec as P


def partner_of(grads):
    pairs = grads.reshape(grads.shape[:-1] + (grads.shape[-1] // 2, 2))
    swapped = jnp.stack([pairs[..., 1], -pairs[..., 0]], axis=-1)
    return swapped.reshape(grads.shape)


def weight_terms(spectra, grads):
    pairs = spectra.reshape(spectra.shape[:-1] + (spectra.shape[-1] // 2, 2))
    partner = partner_of(grads)
    first = jnp.einsum("bmli,bmlq->liq", pairs[..., 0], grads, preferred_element_type=jnp.float32)
    second = jnp.einsum(
        "bmli,bmlq->liq", pairs[..., 1], partner, preferred_element_type=jnp.float32
    )
    return first + second


def on_device(saved_input, grad_output, legendre, quad_weight, mixing_weight):
    analysis = (legendre.astype(jnp.float32) * quad_weight[None, None, :]).astype(jnp.bfloat16)
    spectra = jnp.einsum(
        "mlj,bmjq->bmlq",
        analysis,
        lax.all_to_all(saved_input, "lat", split_axis=1, concat_axis=2, tiled=True),
        preferred_element_type=jnp.float32,
    ).astype(jnp.bfloat16)
    grads = jnp.einsum(
        "mlj,bmjq->bmlq",
        legendre,
        lax.all_to_all(grad_output, "lat", split_axis=1, concat_axis=2, tiled=True),
        preferred_element_type=jnp.float32,
    ).astype(jnp.bfloat16)
    spectra, grad_spectra = (spectra, grads)
    spectra, grad_spectra = (
        lax.all_to_all(spectra, "lat", split_axis=2, concat_axis=1, tiled=True),
        lax.all_to_all(grad_spectra, "lat", split_axis=2, concat_axis=1, tiled=True),
    )
    batch = saved_input.shape[0] * lax.axis_size("dp")
    complete = lax.all_gather(spectra, "chan", axis=3, tiled=True)
    partial_terms = weight_terms(complete, grad_spectra) / batch
    summed = lax.psum_scatter(
        partial_terms.astype(jnp.bfloat16), "dp", scatter_dimension=1, tiled=True
    )
    partner = partner_of(grad_spectra)
    sum_real = jnp.einsum(
        "bmlq,liq->bmli", grad_spectra, mixing_weight, preferred_element_type=jnp.float32
    )
    sum_imag = jnp.einsum(
        "bmlq,liq->bmli", partner, mixing_weight, preferred_element_type=jnp.float32
    )
    terms = jnp.stack([sum_real, sum_imag], axis=-1)
    terms = terms.reshape(terms.shape[:3] + (terms.shape[3] * 2,))
    grad_spec_in = lax.psum_scatter(
        terms.astype(jnp.bfloat16), "chan", scatter_dimension=3, tiled=True
    )
    grad_local = jnp.einsum(
        "mlj,bmlq->bmjq",
        analysis,
        lax.all_to_all(grad_spec_in, "lat", split_axis=1, concat_axis=2, tiled=True),
        preferred_element_type=jnp.float32,
    ).astype(jnp.bfloat16)
    grad_input = lax.all_to_all(grad_local, "lat", split_axis=2, concat_axis=1, tiled=True)
    return (summed, grad_input)


def solution(mesh):
    in_specs = (
        P("dp", None, "lat", "chan"),
        P("dp", None, "lat", "chan"),
        P("lat", None, None),
        P(),
        P("lat", None, "chan"),
    )
    out_specs = (P("lat", "dp", "chan"), P("dp", None, "lat", "chan"))
    return jax.shard_map(
        on_device, mesh=mesh, in_specs=in_specs, out_specs=out_specs, check_vma=False
    )
```

profile of v0, /device:TPU:0, one launch (start us, length us, event | category | flops | bytes accessed | tf_op | source)
XLA Modules:
  0.0 495.2 jit_solution(13949180466964692547)
XLA Ops:
  7.2 5.1 %copy.96 = bf16[1,16,180,512]{3,2,0,1:T(8,128)(2,1)} copy(bf16[1,16,180,512]{3,1,2,0:T(8,128)(2,1)} %param.6) | data formatting | bytes 5898240 | tf_op args[1]
  12.3 6.3 %all-to-all-start.2 = ((bf16[1,16,180,512]{3,2,0,1:T(8,128)(2,1)}), bf16[1,16,180,512]{3,2,0,1:T(8,128)(2,1)S(1)}, u32[]{:S(2)}, u32[]{:S(2)}) async-start(bf16[1,16,180,512]{3,2,0,1:T(8,128)(2,1)} %copy.96), calls=%async_computation.2 | async-start | bytes 6029312 | tf_op jit(solution)/shard_map/all_to_all | solution.py:34
  18.6 5.1 %copy.89 = bf16[1,16,180,512]{3,2,0,1:T(8,128)(2,1)} copy(bf16[1,16,180,512]{3,1,2,0:T(8,128)(2,1)} %param.5) | data formatting | bytes 5898240 | tf_op args[0]
  23.7 62.8 %all-to-all-done.2 = bf16[1,16,180,512]{3,2,0,1:T(8,128)(2,1)S(1)} async-done(((bf16[1,16,180,512]{3,2,0,1:T(8,128)(2,1)}), bf16[1,16,180,512]{3,2,0,1:T(8,128)(2,1)S(1)}, u32[]{:S(2)}, u32[]{:S(2)}) %all-to-all-start.2) | async-done | bytes 2949152 | tf_op jit(solution)/shard_map/all_to_all | solution.py:34
  86.5 0.0 copy-start.1
  86.5 1.6 copy-done.1
  88.1 3.7 all-to-all-start
  91.8 3.8 copy.120
  95.6 4.3 reshape.77
  99.9 3.0 fusion.1
  102.8 1.5 copy.98
  104.3 54.8 %all-to-all-done = bf16[1,16,180,512]{3,2,0,1:T(8,128)(2,1)S(1)} async-done(((bf16[1,16,180,512]{3,2,0,1:T(8,128)(2,1)}), bf16[1,16,180,512]{3,2,0,1:T(8,128)(2,1)S(1)}, u32[]{:S(2)}, u32[]{:S(2)}) %all-to-all-start) | async-done | bytes 2949152 | tf_op jit(solution)/shard_map/all_to_all | solution.py:28
  159.2 4.2 all-to-all-start.3
  163.4 1.9 copy.121
  165.3 0.0 copy-start.2
  165.3 0.0 copy-start.4
  165.3 4.4 reshape.74
  169.7 0.0 copy-done.2
  169.7 0.0 copy-done.4
  169.7 2.6 fusion
  172.3 1.5 copy.91
  173.8 9.3 %all-to-all-done.3 = bf16[1,4,192,512]{3,1,0,2:T(4,128)(2,1)} async-done(((bf16[1,4,192,512]{3,1,0,2:T(4,128)(2,1)}), bf16[1,4,192,512]{3,1,0,2:T(4,128)(2,1)}, u32[]{:S(2)}, u32[]{:S(2)}) %all-to-all-start.3) | async-done | bytes 786464 | tf_op jit(solution)/shard_map/all_to_all | solution.py:40
  183.1 4.2 all-to-all-start.1
  187.3 0.2 all-gather.2.cloned.1.call-start
  187.5 2.8 copy.99
  190.4 3.9 fusion.8
  194.2 5.6 %pad_maximum_fusion = bf16[1,16,48,256,2]{2,4,3,1,0:T(2,128)(2,1)S(1)} fusion(bf16[1,16,48,256,1]{2,4,3,1,0:T(2,128)(2,1)S(1)} %get-tuple-element.13, bf16[1,16,48,256,1]{2,4,3,1,0:T(2,128)(2,1)S(1)} %get-tuple-element.12), kind=kLoop, calls=%fused_computation.7 | loop fusion | flops 1572864 | bytes 1572864 | tf_op jit(solution)/shard_map/stack | solution.py:9
  199.8 3.8 copy.102
  203.6 4.0 copy.103
  207.6 1.3 copy.112
  208.9 0.0 copy-start
  208.9 0.0 all-to-all-done.1
  208.9 1.3 copy.92
  210.3 0.9 copy.93
  211.2 0.0 all-gather.2.cloned.1.call-update
  211.2 0.3 reduce-scatter.5.cloned.1.call-start
  211.5 0.0 copy-done
  211.5 12.0 %fusion.3 = bf16[1,16,48,512,1]{3,1,2,4,0:T(8,128)(2,1)S(1)} fusion(bf16[16,48,512]{2,0,1:T(8,128)(2,1)S(1)} %copy-done, bf16[48,512,512]{2,1,0:T(8,128)(2,1)} %param.9), kind=kOutput, calls=%fused_computation.16 | convolution fusion | flops 403046400 | bytes 26738688 | tf_op jit(solution)/shard_map/bmlq,liq->bmli/dot_general | solution.py:52
  223.5 12.5 %fusion.2 = bf16[1,16,48,512,1]{3,1,2,4,0:T(8,128)(2,1)} fusion(bf16[16,48,512]{2,0,1:T(8,128)(2,1)S(1)} %copy.112, bf16[48,512,512]{2,1,0:T(8,128)(2,1)} %param.9), kind=kOutput, calls=%fused_computation.15 | convolution fusion | flops 403046400 | bytes 26738688 | tf_op jit(solution)/shard_map/bmlq,liq->bmli/dot_general | solution.py:49
  236.0 2.4 pad_maximum_fusion.1
  238.4 8.6 %copy.105 = bf16[1,16,48,512,2]{2,1,4,3,0:T(8,128)(2,1)} copy(bf16[1,16,48,512,2]{3,1,2,4,0:T(8,128)(2,1)} %pad_maximum_fusion.1) | data formatting | bytes 3145728 | tf_op jit(solution)/shard_map/stack | solution.py:55
  247.0 0.0 reduce-scatter.5.cloned.1.call-update
  247.0 0.3 reduce-scatter.3.cloned.1.call-start
  247.3 0.0 all-gather.2.cloned.1.call-done
  247.4 6.1 %copy.94 = bf16[1,16,48,1024]{2,1,3,0:T(8,128)(2,1)} copy(bf16[1,16,48,1024]{3,2,1,0:T(8,128)(2,1)} %all-gather.2.cloned.1.call-done) | data formatting | bytes 3145728 | tf_op jit(solution)/shard_map/all_gather | solution.py:43
  253.4 5.6 %fusion.7 = (bf16[1,16,48,512,1]{2,1,4,3,0:T(8,128)(2,1)}, bf16[1,16,48,512,1]{2,1,4,3,0:T(8,128)(2,1)}) fusion(bf16[1,16,48,512,2]{2,1,4,3,0:T(8,128)(2,1)} %bitcast.79), kind=kLoop, calls=%fused_computation.20 | loop fusion | bytes 3145728 | tf_op jit(solution)/shard_map/slice | solution.py:18
  259.0 3.2 copy.114
  262.2 20.2 %fusion.5 = f32[48,512,512]{2,1,0:T(8,128)} fusion(bf16[16,48,512]{2,0,1:T(8,128)(2,1)S(1)} %copy.112, bf16[1,16,48,512,1]{3,1,2,4,0:T(8,128)(2,1)S(1)} %copy.114), kind=kOutput, calls=%fused_computation.18 | convolution fusion | flops 402653184 | bytes 51904512 | tf_op jit(solution)/shard_map/bmli,bmlq->liq/dot_general | solution.py:16
  282.4 3.2 copy.115
  285.6 26.3 %multiply_convert_fusion = bf16[48,512,512]{2,1,0:T(8,128)(2,1)} fusion(f32[48,512,512]{2,1,0:T(8,128)} %fusion.5, bf16[16,48,512]{2,0,1:T(8,128)(2,1)S(1)} %copy-done, bf16[1,16,48,512,1]{3,1,2,4,0:T(8,128)(2,1)S(1)} %copy.115), kind=kOutput, calls=%fused_computation | convolution fusion | flops 440401920 | bytes 77070336 | tf_op jit(solution)/shard_map/bmli,bmlq->liq/dot_general | solution.py:17
  311.9 0.0 reduce-scatter.3.cloned.1.call-update
  311.9 0.0 copy-start.3
  312.0 0.0 reduce-scatter.5.cloned.1.call-done
  312.0 2.6 copy.106
  314.6 22.4 %all_to_all.96 = bf16[1,16,48,512]{3,2,0,1:T(8,128)(2,1)S(1)} all-to-all(bf16[1,16,48,512]{3,2,0,1:T(8,128)(2,1)S(1)} %copy.106), channel_id=1, replica_groups=mesh['dp'=4,'lat'=4,'chan'=2] {'lat'}, dimensions={1} | all-to-all | bytes 1572864 | tf_op jit(solution)/shard_map/all_to_all | solution.py:63
  337.0 0.1 copy.107
  337.1 0.0 copy-done.3
  337.1 1.0 convert_bitcast_fusion
  338.1 2.3 copy.108
  340.3 67.9 %all_to_all.97 = bf16[1,4,720,512]{3,1,0,2:T(4,128)(2,1)S(1)} all-to-all(bf16[1,4,720,512]{3,1,0,2:T(4,128)(2,1)S(1)} %copy.108), channel_id=1, replica_groups=mesh['dp'=4,'lat'=4,'chan'=2] {'lat'}, dimensions={2} | all-to-all | bytes 5898240 | tf_op jit(solution)/shard_map/all_to_all | solution.py:66
  408.2 0.6 copy.119
  408.8 0.3 copy.110
  409.1 2.6 copy.111
  411.7 77.0 %reduce-scatter.3.cloned.1.call-done = bf16[48,128,512]{2,1,0:T(8,128)(2,1)} async-done(((bf16[48,512,512]{2,1,0:T(8,128)(2,1)}), bf16[48,128,512]{2,1,0:T(8,128)(2,1)}) %reduce-scatter.3.cloned.1.call-update) | async-done | bytes 6291472 | tf_op jit(solution)/shard_map/reduce_scatter | solution.py:45
Async XLA Ops:
  12.3 74.2 %all-to-all-start.2 = ((bf16[1,16,180,512]{3,2,0,1:T(8,128)(2,1)}), bf16[1,16,180,512]{3,2,0,1:T(8,128)(2,1)S(1)}, u32[]{:S(2)}, u32[]{:S(2)}) async-start(bf16[1,16,180,512]{3,2,0,1:T(8,128)(2,1)} %copy.96), calls=%async_computation.2 | async-start | bytes 6029312 | tf_op jit(solution)/shard_map/all_to_all | solution.py:34
  86.5 1.6 copy-start.1
  88.1 71.1 %all-to-all-start = ((bf16[1,16,180,512]{3,2,0,1:T(8,128)(2,1)}), bf16[1,16,180,512]{3,2,0,1:T(8,128)(2,1)S(1)}, u32[]{:S(2)}, u32[]{:S(2)}) async-start(bf16[1,16,180,512]{3,2,0,1:T(8,128)(2,1)} %copy.89), calls=%async_computation | async-start | bytes 6029312 | tf_op jit(solution)/shard_map/all_to_all | solution.py:28
  159.2 23.9 %all-to-all-start.3 = ((bf16[1,4,192,512]{3,1,0,2:T(4,128)(2,1)}), bf16[1,4,192,512]{3,1,0,2:T(4,128)(2,1)}, u32[]{:S(2)}, u32[]{:S(2)}) async-start(bf16[1,4,192,512]{3,1,0,2:T(4,128)(2,1)} %copy.98), calls=%async_computation.3 | async-start | bytes 1572864 | tf_op jit(solution)/shard_map/all_to_all | solution.py:40
  165.3 4.4 copy-start.2
  165.3 4.4 copy-start.4
  183.1 25.8 %all-to-all-start.1 = ((bf16[1,4,192,512]{3,1,0,2:T(4,128)(2,1)}), bf16[1,4,192,512]{3,1,0,2:T(4,128)(2,1)}, u32[]{:S(2)}, u32[]{:S(2)}) async-start(bf16[1,4,192,512]{3,1,0,2:T(4,128)(2,1)} %copy.91), calls=%async_computation.1 | async-start | bytes 1572864 | tf_op jit(solution)/shard_map/all_to_all | solution.py:39
  187.3 60.0 %all-gather.2.cloned.1.call-start = ((), (), s32[]{:S(2)}) async-start(), calls=%async_computation.8 | async-start | bytes 2359296 | tf_op jit(solution)/shard_map/all_gather | solution.py:43
  208.9 2.6 copy-start
  211.2 100.7 %reduce-scatter.5.cloned.1.call-start = ((), (), s32[]{:S(2)}) async-start(), calls=%async_computation.10 | async-start | bytes 6291456 | tf_op jit(solution)/shard_map/reduce_scatter | solution.py:57
  247.0 241.7 %reduce-scatter.3.cloned.1.call-start = ((), (), s32[]{:S(2)}) async-start(), calls=%async_computation.9 | async-start | bytes 31457280 | tf_op jit(solution)/shard_map/reduce_scatter | solution.py:45
  311.9 25.1 %copy-start.3 = (bf16[4,192,720]{2,1,0:T(8,128)(2,1)S(1)}, bf16[4,192,720]{2,1,0:T(8,128)(2,1)}, u32[]{:S(2)}) copy-start(bf16[4,192,720]{2,1,0:T(8,128)(2,1)} %param.7) | copy-start | bytes 3317764
Sparse Core Ops, SparseCore 0:
  211.4 28.3 all-gather.1
  247.1 55.5 reduce-scatter.4
  312.1 176.6 reduce-scatter.2
where the time goes:
time: 496 us; the launch traced here: 495 us
  waiting for transfers between devices  204 us (41%)
  blocking collectives  90.3 us (18%)
  local copies, waits for them, and re-layouts  78.4 us (16%)
  matrix products  77.5 us (16%)
  starting transfers between devices  19.2 us (4%)
  between operations  13.9 us (3%)
  other arithmetic  11.9 us (2%)
    reduce_scatter x1, waiting for transfers between devices, on_device(): lax.psum_scatter(partial_terms.astype(jnp.bfloat16), 'dp', scatter_dimens...  77 us
    all_to_all x1, blocking collectives, on_device(): lax.all_to_all(grad_local, 'lat', split_axis=2, concat_axis=1, tiled=True)  67.9 us
    all_to_all x1, waiting for transfers between devices, on_device(): lax.all_to_all(grad_output, 'lat', split_axis=1, concat_axis=2, tiled=True)  62.8 us
    all_to_all x1, waiting for transfers between devices, on_device(): lax.all_to_all(saved_input, 'lat', split_axis=1, concat_axis=2, tiled=True)  54.8 us
    dot_general x1, matrix products, weight_terms(): jnp.einsum('bmli,bmlq->liq', pairs[..., 1], partner, preferred_element_ty...  26.3 us
    all_to_all x1, blocking collectives, on_device(): lax.all_to_all(grad_spec_in, 'lat', split_axis=1, concat_axis=2, tiled=True)  22.4 us
    unnamed x15, local copies, waits for them, and re-layouts  20.8 us
    dot_general x1, matrix products, weight_terms(): jnp.einsum('bmli,bmlq->liq', pairs[..., 0], grads, preferred_element_type...  20.2 us
  transfers between devices with their start and end apart: 7, of which 4 were waited for; matrix products, arithmetic and copies ran while one was open for 32% of the time, Pallas kernels for 0%

commit v1 on v0

v1 whole, which is shorter than its diff:
```python
import jax
import jax.numpy as jnp
from jax import lax
from jax.sharding import PartitionSpec as P

BF = jnp.bfloat16
F32 = jnp.float32


def lane_swap(width):
    row = lax.broadcasted_iota(jnp.int32, (width, width), 0)
    col = lax.broadcasted_iota(jnp.int32, (width, width), 1)
    up = (row == col + 1) & (col % 2 == 0)
    down = (col == row + 1) & (row % 2 == 0)
    return (up.astype(F32) - down.astype(F32)).astype(BF)


def to_planes(width):
    row = lax.broadcasted_iota(jnp.int32, (width, width), 0)
    col = lax.broadcasted_iota(jnp.int32, (width, width), 1)
    return ((row // 2 + (row % 2) * (width // 2)) == col).astype(BF)


def lanes(x, matrix):
    return jnp.einsum("...q,qp->...p", x, matrix, preferred_element_type=F32).astype(BF)


def shifted(x, axis, step):
    n = lax.axis_size(axis)
    return lax.ppermute(x, axis, [(i, (i + step) % n) for i in range(n)])


def pick(x, index):
    return lax.dynamic_index_in_dim(x, index, 0, keepdims=False)


def on_device(saved_input, grad_output, legendre, quad_weight, mixing_weight):
    local_lat = saved_input.shape[2]
    width = saved_input.shape[3]
    own_m, n_deg, n_lat = legendre.shape
    lat_size = lax.axis_size("lat")
    n_dp, n_chan = lax.axis_size("dp"), lax.axis_size("chan")
    my_dp, my_chan = lax.axis_index("dp"), lax.axis_index("chan")
    batch = saved_input.shape[0] * n_dp
    swap, planes = lane_swap(width), to_planes(width)

    share = 2 if own_m % 2 == 0 and n_dp % 2 == 0 else 1
    per = own_m // share
    half_of = my_dp % share
    orders = pick(legendre.reshape(share, per * n_deg, n_lat), half_of)
    by_lat = orders.T.reshape(lat_size, local_lat, per * n_deg)
    by_lat = lax.all_to_all(by_lat, "lat", split_axis=0, concat_axis=0, tiled=True)
    held = [by_lat]
    if share == 2:
        other = lax.ppermute(by_lat, "dp", [(i, i ^ 1) for i in range(n_dp)])
        first = half_of == 0
        held = [jnp.where(first, by_lat, other), jnp.where(first, other, by_lat)]
    held = [
        jnp.transpose(x.reshape(lat_size, local_lat, per, n_deg), (0, 2, 3, 1))
        for x in held
    ]
    table = jnp.concatenate(held, axis=1).reshape(lat_size * own_m, n_deg, local_lat)
    weights = lax.dynamic_slice_in_dim(
        quad_weight, lax.axis_index("lat") * local_lat, local_lat
    )
    analysis = (table.astype(F32) * weights[None, None, :]).astype(BF)

    def spectrum(tab, grid):
        part = jnp.einsum("mlj,bmjq->lbmq", tab, grid, preferred_element_type=F32)
        return lax.psum_scatter(part.astype(BF), "lat", scatter_dimension=0, tiled=True)

    grads = spectrum(table, grad_output)
    spectra = spectrum(analysis, saved_input)
    n_l, n_b, n_m = grads.shape[:3]
    rows = n_b * n_m

    flat = grads.reshape(n_l, rows, width)
    both = jnp.concatenate([flat, lanes(flat, swap)], axis=1)
    n_i = mixing_weight.shape[1]
    mine = n_i // n_chan
    split_weight = mixing_weight.reshape(n_l, n_chan, mine, width)
    terms = jnp.einsum("lrq,lciq->clri", both, split_weight, preferred_element_type=F32)
    terms = terms.astype(BF)
    total = pick(terms, my_chan).astype(F32)
    for step in range(1, n_chan):
        sent = pick(terms, (my_chan + step) % n_chan)
        total = total + shifted(sent, "chan", step).astype(F32)
    total = total.astype(BF)
    half = lanes_join(total.reshape(n_l, 2, rows, mine), planes)
    everyone = [flat] + [shifted(flat, "dp", step) for step in range(1, n_dp)]

    spectra, half, *everyone = lax.optimization_barrier((spectra, half, *everyone))
    spec_in = lax.all_gather(half, "lat", axis=0, tiled=True).reshape(-1, n_b, n_m, width)
    grad_input = jnp.einsum(
        "mlj,lbmq->bmjq", analysis, spec_in, preferred_element_type=F32
    ).astype(BF)

    block = n_i // n_dp
    size = min(block, mine)
    per_chan, per_block = mine // size, block // size
    planar = lanes(spectra.reshape(n_l, rows, width), planes)
    pieces = jnp.moveaxis(planar.reshape(n_l, rows, 2, per_chan, size), 3, 0)
    pieces = pieces.reshape(per_chan, n_l, rows, 2 * size)
    pieces = jnp.concatenate(
        [pieces] + [shifted(pieces, "chan", step) for step in range(1, n_chan)]
    )

    def piece(index):
        place = (my_chan - index // per_chan) % n_chan
        return pick(pieces, place * per_chan + index % per_chan)

    def block_of(owner):
        parts = [piece(owner * per_block + t) for t in range(per_block)]
        return jnp.stack(parts)

    ours = [block_of(my_dp)]
    for step in range(1, n_dp):
        ours.append(shifted(block_of((my_dp + step) % n_dp), "dp", step))
    left = jnp.stack(ours).reshape(n_dp, per_block, n_l, rows, 2, size)
    right = jnp.stack(everyone)
    right = jnp.stack([right, lanes(right, swap)])
    grad_weight = jnp.einsum(
        "dtlrpi,pdlrq->ltiq", left, right, preferred_element_type=F32
    ) / batch
    return (grad_weight.reshape(n_l, block, width).astype(BF), grad_input)


def lanes_join(parts, planes):
    n = parts.shape[-1]
    real = jnp.einsum("lri,qi->lrq", parts[:, 0], planes[:, :n], preferred_element_type=F32)
    imag = jnp.einsum("lri,qi->lrq", parts[:, 1], planes[:, n:], preferred_element_type=F32)
    return (real + imag).astype(BF)


def solution(mesh):
    in_specs = (
        P("dp", None, "lat", "chan"),
        P("dp", None, "lat", "chan"),
        P("lat", None, None),
        P(),
        P("lat", None, "chan"),
    )
    out_specs = (P("lat", "dp", "chan"), P("dp", None, "lat", "chan"))
    return jax.shard_map(
        on_device, mesh=mesh, in_specs=in_specs, out_specs=out_specs, check_vma=False
    )
```

time: 496 us -> 257 us (0.52)
  waiting for transfers between devices: 204 us -> 120 us
  blocking collectives: 90.3 us -> 21.7 us
  local copies, waits for them, and re-layouts: 78.4 us -> 22.2 us
  matrix products: 77.5 us -> 55.3 us
  starting transfers between devices: 19.2 us -> 9.19 us
    all_to_all x4 -> x0, waiting for transfers between devices: 127 us -> none  [the longest x1 62.8 us: on_device(): lax.all_to_all(grad_output, 'lat', split_axis=1, concat_axis=2, tiled=True)]
    all_to_all x2 -> x1, blocking collectives: 90.3 us -> 21.7 us  [on_device(): lax.all_to_all(by_lat, 'lat', split_axis=0, concat_axis=0, tiled=True)]
    ppermute x0 -> x9, waiting for transfers between devices: none -> 39.6 us  [the longest x8 37.3 us: shifted(): return lax.ppermute(x, axis, [(i, (i + step) % n) for i in range(n)])]
    dot_general x7 -> x10, matrix products: 77.5 us -> 55.3 us  [the longest x1 13.5 us: on_device(): jnp.einsum('dtlrpi,pdlrq->ltiq', left, right, preferred_element_type=F32)]
    another operation x5 -> x8, local copies, waits for them, and re-layouts: 22 us -> 0.59 us  [on_device(): left = jnp.stack(ours).reshape(n_dp, per_block, n_l, rows, 2, size)]
    all_to_all x4 -> x0, starting transfers between devices: 18.4 us -> none  [the longest x1 6.35 us: on_device(): lax.all_to_all(grad_output, 'lat', split_axis=1, concat_axis=2, tiled=True)]
    unnamed x15 -> x12, local copies, waits for them, and re-layouts: 20.8 us -> 5.43 us
    all_to_all x8 -> x1, local copies, waits for them, and re-layouts: 11.7 us -> 1.02 us  [on_device(): lax.all_to_all(by_lat, 'lat', split_axis=0, concat_axis=0, tiled=True)]
  transfers between devices with their start and end apart: 7 -> 12, of which waited for: 4 -> 9; matrix products, arithmetic and copies ran while one was open for 32% -> 23% of each run, Pallas kernels for 0% -> 0%
where the time goes in v1:
time: 257 us; the launch traced here: 256 us
  waiting for transfers between devices  120 us (47%)
  matrix products  55.3 us (22%)
  local copies, waits for them, and re-layouts  22.2 us (9%)
  blocking collectives  21.7 us (8%)
  between operations  14 us (5%)
  other arithmetic  13.9 us (5%)
  starting transfers between devices  9.19 us (4%)
    reduce_scatter x2, waiting for transfers between devices, spectrum(): lax.psum_scatter(part.astype(BF), 'lat', scatter_dimension=0, tiled=True)  73.7 us
    ppermute x8, waiting for transfers between devices, shifted(): return lax.ppermute(x, axis, [(i, (i + step) % n) for i in range(n)])  37.3 us
    all_to_all x1, blocking collectives, on_device(): lax.all_to_all(by_lat, 'lat', split_axis=0, concat_axis=0, tiled=True)  21.7 us
    dot_general x1, matrix products, on_device(): jnp.einsum('dtlrpi,pdlrq->ltiq', left, right, preferred_element_type=F32)  13.5 us
    dot_general x1, matrix products, on_device(): jnp.einsum('lrq,lciq->clri', both, split_weight, preferred_element_type=F32)  13 us
    dot_general x2, matrix products, spectrum(): part = jnp.einsum('mlj,bmjq->lbmq', tab, grid, preferred_element_type=F32)  13 us
    ppermute x8, starting transfers between devices, shifted(): return lax.ppermute(x, axis, [(i, (i + step) % n) for i in range(n)])  8.88 us
    dot_general x3, matrix products, lanes(): jnp.einsum('...q,qp->...p', x, matrix, preferred_element_type=F32)  7.75 us
  transfers between devices with their start and end apart: 12, of which 9 were waited for; matrix products, arithmetic and copies ran while one was open for 23% of the time, Pallas kernels for 0%

profile of v1, /device:TPU:0, one launch (start us, length us, event | category | flops | bytes accessed | tf_op | source)
XLA Modules:
  0.0 256.2 jit_solution(12533947805916880893)
XLA Ops:
  7.2 0.0 reduce-scatter.5.cloned.1.call-start
  7.2 1.3 constant_dynamic-slice_fusion.4
  8.5 1.0 copy.36
  9.5 2.0 reshape.78
  11.5 21.7 %all_to_all.5 = bf16[4,180,384]{2,1,0:T(8,128)(2,1)S(1)} all-to-all(bf16[4,180,384]{2,1,0:T(8,128)(2,1)} %reshape.78), channel_id=1, replica_groups=mesh['dp'=4,'lat'=4,'chan'=2] {'lat'}, dimensions={0} | all-to-all | bytes 1105920 | tf_op jit(solution)/shard_map/all_to_all | solution.py:52
  33.2 1.0 copy.37
  34.2 2.3 collective-permute-done
  36.5 2.2 broadcast_select_fusion.1
  38.7 2.3 reshape.79
  41.1 2.3 reshape.80
  43.4 3.0 %pad_maximum_fusion.2 = bf16[4,4,192,180]{2,1,3,0:T(4,128)(2,1)S(1)} fusion(bf16[4,2,192,180]{2,1,3,0:T(2,128)(2,1)} %bitcast.111, bf16[4,2,192,180]{2,1,3,0:T(2,128)(2,1)} %bitcast.110), kind=kLoop, calls=%fused_computation.32 | loop fusion | flops 2211840 | bytes 2211840 | tf_op jit(solution)/shard_map/concatenate | solution.py:62
  46.4 0.2 copy.40
  46.7 1.1 copy-done.2
  47.8 5.5 %convert_bitcast_fusion.1 = bf16[192,1,16,512]{3,0,2,1:T(8,128)(2,1)} fusion(bf16[16,192,180]{1,2,0:T(8,128)(2,1)S(1)} %bitcast.97, bf16[16,180,512]{2,0,1:T(8,128)(2,1)S(1)} %bitcast.95), kind=kOutput, calls=%fused_computation.9 | convolution fusion | flops 567803904 | bytes 7200768 | tf_op jit(solution)/shard_map/mlj,bmjq->lbmq/dot_general | solution.py:69
  53.3 0.0 reduce-scatter.3.cloned.1.call-start
  53.4 0.9 dynamic_slice.24
  54.2 0.5 copy-done.3
  54.7 7.5 %convert_bitcast_fusion.2 = bf16[192,1,16,512]{3,0,2,1:T(8,128)(2,1)} fusion(bf16[16,180,512]{2,0,1:T(8,128)(2,1)} %bitcast.109, bf16[16,192,180]{1,2,0:T(8,128)(2,1)S(1)} %bitcast.99, f32[180]{0:T(256)S(1)} %dynamic_slice.24), kind=kOutput, calls=%fused_computation.10 | convolution fusion | flops 569462784 | bytes 7201488 | tf_op jit(solution)/shard_map/mlj,bmjq->lbmq/dot_general | solution.py:69
  62.2 0.2 all-gather.2.cloned.1.call-start
  62.5 50.6 %reduce-scatter.5.cloned.1.call-done = bf16[48,1,16,512]{3,0,2,1:T(8,128)(2,1)} async-done(((bf16[192,1,16,512]{3,0,2,1:T(8,128)(2,1)}), bf16[48,1,16,512]{3,0,2,1:T(8,128)(2,1)}) %reduce-scatter.5.cloned.1.call-update) | async-done | bytes 786448 | tf_op jit(solution)/shard_map/reduce_scatter | solution.py:70
  113.1 2.0 convolution_convert_fusion.1
  115.0 1.3 maximum_bitcast_fusion
  116.3 13.0 %convolution_convert_fusion = bf16[48,32,2,256]{3,1,2,0:T(8,128)(2,1)S(1)} fusion(bf16[48,2,256,512]{3,2,1,0:T(8,128)(2,1)} %bitcast.96, bf16[48,32,512,1]{2,0,1,3:T(8,128)(2,1)} %maximum_bitcast_fusion), kind=kOutput, calls=%fused_computation.17 | convolution fusion | flops 806092800 | bytes 28311552 | tf_op jit(solution)/shard_map/lrq,lciq->clri/dot_general | solution.py:82
  129.3 1.0 dynamic-slice_bitcast_fusion
  130.3 1.5 collective-permute-start.1
  131.8 0.7 fusion.26
  132.4 0.1 collective-permute-start.2
  132.5 1.5 collective-permute-start.3
  134.0 1.4 collective-permute-start.4
  135.4 14.1 %collective-permute-done.1 = bf16[48,32,256]{2,1,0:T(8,128)(2,1)} collective-permute-done((bf16[48,32,256]{2,1,0:T(8,128)(2,1)}, bf16[48,32,256]{2,1,0:T(8,128)(2,1)}, u32[]{:S(2)}, u32[]{:S(2)}) %collective-permute-start.1) | collective-permute-done | bytes 786464 | tf_op jit(solution)/shard_map/ppermute | solution.py:30
  149.5 1.4 fusion.23
  150.9 0.4 fusion.34
  151.4 1.3 add_convert_fusion
  152.6 23.0 %reduce-scatter.3.cloned.1.call-done = bf16[48,1,16,512]{3,0,2,1:T(8,128)(2,1)} async-done(((bf16[192,1,16,512]{3,0,2,1:T(8,128)(2,1)}), bf16[48,1,16,512]{3,0,2,1:T(8,128)(2,1)}) %reduce-scatter.3.cloned.1.call-update) | async-done | bytes 786448 | tf_op jit(solution)/shard_map/reduce_scatter | solution.py:70
  175.7 0.0 all-gather.2.cloned.1.call-update
  175.7 2.0 convolution_convert_fusion.2
  177.8 0.2 reshape.88
  178.0 0.5 copy.89
  178.4 1.4 reshape.89
  179.8 1.5 collective-permute-start.5
  181.3 1.2 constant_dynamic-update-slice_fusion.1
  182.5 3.8 %convert_bitcast_fusion = bf16[1,4,48,16,512]{4,2,3,1,0:T(8,128)(2,1)S(1)} fusion(bf16[1,48,16,512]{3,1,2,0:T(8,128)(2,1)} %bitcast.32, bf16[1,48,16,512]{3,1,2,0:T(8,128)(2,1)} %bitcast.31, bf16[1,48,16,512]{3,1,2,0:T(8,128)(2,1)} %bitcast.30, bf16[1,48,16,512]{3,1,2,0:T(8,128)(2,1)S(1)} %bitcast.104, s32[512]{0:T(512)S(1)} %get-tuple-element.28, ...), kind=kOutput, calls=%fused_computation.8 | convolution fusion | flops 1620049920 | bytes 6298112 | tf_op jit(solution)/shard_map/...q,qp->...p/dot_general | solution.py:25
  186.3 12.7 %collective-permute-done.5 = bf16[2,48,16,256]{3,2,1,0:T(8,128)(2,1)} collective-permute-done((bf16[2,48,16,256]{3,2,1,0:T(8,128)(2,1)}, bf16[2,48,16,256]{3,2,1,0:T(8,128)(2,1)}, u32[]{:S(2)}, u32[]{:S(2)}) %collective-permute-start.5) | collective-permute-done | bytes 786464 | tf_op jit(solution)/shard_map/ppermute | solution.py:30
  199.0 1.2 constant_dynamic-update-slice_fusion
  200.2 1.0 constant_dynamic-slice_fusion.3
  201.2 1.5 collective-permute-start.7
  202.7 1.5 collective-permute-start.8
  204.2 2.0 fusion.31
  206.2 3.2 %pad_maximum_fusion = bf16[2,4,48,16,512]{4,2,3,1,0:T(8,128)(2,1)} fusion(bf16[1,4,48,16,512]{4,2,3,1,0:T(8,128)(2,1)S(1)} %convert_bitcast_fusion, bf16[1,4,48,16,512]{4,2,3,1,0:T(8,128)(2,1)S(1)} %fusion.31), kind=kLoop, calls=%fused_computation.2 | loop fusion | flops 3145728 | bytes 12582912 | tf_op jit(solution)/shard_map/stack | solution.py:121
  209.4 0.1 stack.41
  209.5 0.1 copy.48
  209.6 2.7 %collective-permute-done.6 = bf16[1,48,16,256]{3,2,1,0:T(8,128)(2,1)S(1)} collective-permute-done((bf16[1,48,16,256]{3,2,1,0:T(8,128)(2,1)}, bf16[1,48,16,256]{3,2,1,0:T(8,128)(2,1)S(1)}, u32[]{:S(2)}, u32[]{:S(2)}) %collective-permute-start.6) | collective-permute-done | bytes 393248 | tf_op jit(solution)/shard_map/ppermute | solution.py:30
  212.3 0.1 stack.42
  212.4 0.1 copy.49
  212.4 1.0 collective-permute-done.7
  213.4 0.1 stack.43
  213.5 0.1 copy.50
  213.6 6.8 %collective-permute-done.8 = bf16[1,48,16,256]{3,2,1,0:T(8,128)(2,1)S(1)} collective-permute-done((bf16[1,48,16,256]{3,2,1,0:T(8,128)(2,1)}, bf16[1,48,16,256]{3,2,1,0:T(8,128)(2,1)S(1)}, u32[]{:S(2)}, u32[]{:S(2)}) %collective-permute-start.8) | collective-permute-done | bytes 393248 | tf_op jit(solution)/shard_map/ppermute | solution.py:30
  220.4 0.1 stack.44
  220.5 0.1 copy.51
  220.6 13.5 %fusion = bf16[48,128,512]{2,1,0:T(8,128)(2,1)} fusion(bf16[2,4,48,16,512]{4,2,3,1,0:T(8,128)(2,1)} %pad_maximum_fusion, bf16[1,1,48,16,2,128]{5,3,4,2,0,1:T(8,128)(2,1)S(1)} %copy.51, bf16[1,1,48,16,2,128]{5,3,4,2,0,1:T(8,128)(2,1)S(1)} %copy.50, bf16[1,1,48,16,2,128]{5,3,4,2,0,1:T(8,128)(2,1)S(1)} %copy.49, bf16[1,1,48,16,2,128]{5,3,4,2,0,1:T(8,128)(2,1)S(1)} %copy.48), kind=kOutput, calls=%fused_computation.1 | convolution fusion | flops 813957120 | bytes 14155776 | tf_op jit(solution)/shard_map/dtlrpi,pdlrq->ltiq/dot_general | solution.py:122
  234.0 6.6 %all-gather.2.cloned.1.call-done = bf16[192,16,512]{2,1,0:T(8,128)(2,1)} async-done(((bf16[48,16,512]{2,1,0:T(8,128)(2,1)}), bf16[192,16,512]{2,1,0:T(8,128)(2,1)}) %all-gather.2.cloned.1.call-update) | async-done | bytes 3145744 | tf_op jit(solution)/shard_map/all_gather | solution.py:93
  240.7 6.4 %convert_bitcast_fusion.3 = bf16[1,16,180,512]{3,2,1,0:T(8,128)(2,1)S(1)} fusion(bf16[192,16,512]{2,1,0:T(8,128)(2,1)} %all-gather.2.cloned.1.call-done, bf16[16,192,180]{1,2,0:T(8,128)(2,1)} %bitcast.98, f32[180]{0:T(256)S(1)} %dynamic_slice.24), kind=kOutput, calls=%fused_computation.15 | convolution fusion | flops 569364480 | bytes 7201488 | tf_op jit(solution)/shard_map/mlj,lbmq->bmjq/dot_general | solution.py:94
  247.0 2.6 %copy.56 = bf16[1,16,180,512]{3,1,2,0:T(8,128)(2,1)} copy(bf16[1,16,180,512]{3,2,1,0:T(8,128)(2,1)S(1)} %convert_bitcast_fusion.3) | data formatting | bytes 5898240
  (20 shorter events, 0.1 us)
Async XLA Ops:
  7.2 39.5 %copy-start = (bf16[1,16,180,512]{3,1,2,0:T(8,128)(2,1)S(1)}, bf16[1,16,180,512]{3,1,2,0:T(8,128)(2,1)}, u32[]{:S(2)}) copy-start(bf16[1,16,180,512]{3,1,2,0:T(8,128)(2,1)} %param.6) | copy-start | bytes 8847364
  7.2 105.9 %reduce-scatter.5.cloned.1.call-start = ((), (), s32[]{:S(2)}) async-start(), calls=%async_computation.4 | async-start | bytes 3932160 | tf_op jit(solution)/shard_map/reduce_scatter | solution.py:70
  34.2 2.3 collective-permute-start
  46.7 1.1 copy-start.2
  53.3 1.4 copy-start.3
  53.3 122.4 %reduce-scatter.3.cloned.1.call-start = ((), (), s32[]{:S(2)}) async-start(), calls=%async_computation.3 | async-start | bytes 3932160 | tf_op jit(solution)/shard_map/reduce_scatter | solution.py:70
  62.2 178.5 %all-gather.2.cloned.1.call-start = ((), (), s32[]{:S(2)}) async-start(), calls=%async_computation.5 | async-start | bytes 3932160 | tf_op jit(solution)/shard_map/all_gather | solution.py:93
  113.1 2.0 copy-start.4
  130.3 19.2 %collective-permute-start.1 = (bf16[48,32,256]{2,1,0:T(8,128)(2,1)}, bf16[48,32,256]{2,1,0:T(8,128)(2,1)}, u32[]{:S(2)}, u32[]{:S(2)}) collective-permute-start(bf16[48,32,256]{2,1,0:T(8,128)(2,1)} %dynamic-slice_bitcast_fusion), channel_id=1, source_target_pairs={{0,1},{1,0},{2,3},{3,2},{4,5},{5,4},{6,7},{7,6},{8,9},{9,8},{10,11... | collective-permute-start | bytes 2359304 | tf_op jit(solution)/shard_map/ppermute | solution.py:30
  132.4 43.3 %collective-permute-start.2 = (bf16[48,16,512]{2,0,1:T(8,128)(2,1)S(1)}, bf16[48,16,512]{2,0,1:T(8,128)(2,1)}, u32[]{:S(2)}, u32[]{:S(2)}) collective-permute-start(bf16[48,16,512]{2,0,1:T(8,128)(2,1)S(1)} %bitcast.101), channel_id=1, source_target_pairs={{0,8},{8,16},{16,24},{24,0},{1,9},{9,17},{17,25},{25,1},{2,10},{10... | collective-permute-start | bytes 2359304 | tf_op jit(solution)/shard_map/ppermute | solution.py:30
  132.5 43.2 %collective-permute-start.3 = (bf16[48,16,512]{2,0,1:T(8,128)(2,1)S(1)}, bf16[48,16,512]{2,0,1:T(8,128)(2,1)}, u32[]{:S(2)}, u32[]{:S(2)}) collective-permute-start(bf16[48,16,512]{2,0,1:T(8,128)(2,1)S(1)} %bitcast.102), channel_id=1, source_target_pairs={{0,16},{8,24},{16,0},{24,8},{1,17},{9,25},{17,1},{25,9},{2,18},{10... | collective-permute-start | bytes 2359304 | tf_op jit(solution)/shard_map/ppermute | solution.py:30
  134.0 41.7 %collective-permute-start.4 = (bf16[48,16,512]{2,0,1:T(8,128)(2,1)S(1)}, bf16[48,16,512]{2,0,1:T(8,128)(2,1)}, u32[]{:S(2)}, u32[]{:S(2)}) collective-permute-start(bf16[48,16,512]{2,0,1:T(8,128)(2,1)S(1)} %bitcast.103), channel_id=1, source_target_pairs={{0,24},{8,0},{16,8},{24,16},{1,25},{9,1},{17,9},{25,17},{2,26},{10... | collective-permute-start | bytes 2359304 | tf_op jit(solution)/shard_map/ppermute | solution.py:30
  179.8 19.2 %collective-permute-start.5 = (bf16[2,48,16,256]{3,2,1,0:T(8,128)(2,1)}, bf16[2,48,16,256]{3,2,1,0:T(8,128)(2,1)}, u32[]{:S(2)}, u32[]{:S(2)}) collective-permute-start(bf16[2,48,16,256]{3,2,1,0:T(8,128)(2,1)} %reshape.89), channel_id=1, source_target_pairs={{0,1},{1,0},{2,3},{3,2},{4,5},{5,4},{6,7},{7,6},{8,9},{9,8},{10,11... | collective-permute-start | bytes 2359304 | tf_op jit(solution)/shard_map/ppermute | solution.py:30
  201.2 11.0 %collective-permute-start.6 = (bf16[1,48,16,256]{3,2,1,0:T(8,128)(2,1)}, bf16[1,48,16,256]{3,2,1,0:T(8,128)(2,1)S(1)}, u32[]{:S(2)}, u32[]{:S(2)}) collective-permute-start(bf16[1,48,16,256]{3,2,1,0:T(8,128)(2,1)} %get-tuple-element.23), channel_id=1, source_target_pairs={{0,8},{8,16},{16,24},{24,0},{1,9},{9,17},{17,25},{25,1},{2,10},{10... | collective-permute-start | bytes 1179656 | tf_op jit(solution)/shard_map/ppermute | solution.py:30
  201.2 12.2 %collective-permute-start.7 = (bf16[1,48,16,256]{3,2,1,0:T(8,128)(2,1)}, bf16[1,48,16,256]{3,2,1,0:T(8,128)(2,1)S(1)}, u32[]{:S(2)}, u32[]{:S(2)}) collective-permute-start(bf16[1,48,16,256]{3,2,1,0:T(8,128)(2,1)} %get-tuple-element.22), channel_id=1, source_target_pairs={{0,16},{8,24},{16,0},{24,8},{1,17},{9,25},{17,1},{25,9},{2,18},{10... | collective-permute-start | bytes 1179656 | tf_op jit(solution)/shard_map/ppermute | solution.py:30
  202.7 17.7 %collective-permute-start.8 = (bf16[1,48,16,256]{3,2,1,0:T(8,128)(2,1)}, bf16[1,48,16,256]{3,2,1,0:T(8,128)(2,1)S(1)}, u32[]{:S(2)}, u32[]{:S(2)}) collective-permute-start(bf16[1,48,16,256]{3,2,1,0:T(8,128)(2,1)} %get-tuple-element.21), channel_id=1, source_target_pairs={{0,24},{8,0},{16,8},{24,16},{1,25},{9,1},{17,9},{25,17},{2,26},{10... | collective-permute-start | bytes 1179656 | tf_op jit(solution)/shard_map/ppermute | solution.py:30
  240.7 9.0 %copy-start.1 = (bf16[1,16,180,512]{3,1,2,0:T(8,128)(2,1)S(1)}, bf16[1,16,180,512]{3,1,2,0:T(8,128)(2,1)}, u32[]{:S(2)}) copy-start(bf16[1,16,180,512]{3,1,2,0:T(8,128)(2,1)} %param.6) | copy-start | bytes 8847364
Sparse Core Ops, SparseCore 0:
  53.4 59.5 reduce-scatter.4
  115.4 60.2 reduce-scatter.2
  177.3 63.3 all-gather.1
